TPU v7x, 32 devices: a whole 2x2x4 slice. The times are simulated.
32 devices in a mesh: mem: 4 (over x, core), col: 8 (over z, y).
Axes of the slice: x: 2, y: 2, z: 4, core: 2. Of those that a mesh axis runs over, the one named last changes fastest.
Arguments:
- prior: float32 [80, 2, 294912], P('mem', None, 'col'), may hold values from -15 to 15
- posterior: float32 [80, 2, 294912], P('mem', None, 'col'), may hold values from -8 to 8
- control: float32 [2, 294912], P(None, 'col'), may hold values from -4 to 4
- rtps_alpha: float32 [2], replicated, may hold values from 0.5 to 0.95
Outputs:
- analysis: float32 [80, 2, 294912], P('mem', None, 'col')
- spread_stats: float32 [4, 2], replicated
All inputs are finite; a program needn't handle non-finite values.
Results may differ from a plain program's by a relative error of at most 0.0001.
Values sent between devices are 32-bit elements; how exact they have to be, the bound alone decides.
A program may use at most 64 MiB of HBM per device.

v0:
```python
import functools
import math

import jax
import jax.numpy as jnp
from jax import lax
from jax.experimental import pallas as pl
from jax.experimental.pallas import tpu as pltpu
from jax.sharding import PartitionSpec as P

NLON = 1536
LANES = 128
PARTS = 3
AHEAD = 4

spread_floor = 0.04


def kernel(
    sizes,
    alpha_hbm,
    prior_hbm,
    post_hbm,
    control_hbm,
    out_ref,
    stats_ref,
    prior_v,
    control_v,
    send_a,
    recv_a,
    sum_x,
    recv_x,
    sum_own,
    field,
    slots,
    weight_v,
    alpha_ref,
    alpha_sem,
    load_sem,
    control_sem,
    a_send,
    a_recv,
    x_send,
    x_recv,
    r_send,
    r_recv,
    d_send,
    d_recv,
    t_send,
    t_recv,
    token,
):
    groups, tiles_n, col_tiles, lat_tiles, lat_count, weight_sum = sizes
    count, rows, _ = prior_v.shape
    members = count * groups
    quarter = rows // 4
    piece = quarter // PARTS
    me = lax.axis_index("mem")
    tile = lax.axis_index("col")
    core = lax.rem(me, 2)
    chip = lax.div(me, 2)
    other_core = chip * 2 + (1 - core)
    other_chip = (1 - chip) * 2 + core
    own = core * 2 + chip
    mine_far = core * 2 + (1 - chip)
    pair_far = (1 - core) * 2 + (1 - chip)
    pair_near = (1 - core) * 2 + chip

    def start(q, s):
        return pl.multiple_of(q * quarter + s * piece, 8)

    order = []
    for far, near in ((pair_far, mine_far), (pair_near, own)):
        for s in range(PARTS):
            order += [(far, s), (near, s)]
    loads = []
    for i, (q, s) in enumerate(order):
        span = pl.ds(start(q, s), piece)
        pair = []
        for k, (src, dst) in enumerate(((prior_hbm, prior_v), (post_hbm, out_ref))):
            copy = pltpu.make_async_copy(src.at[:, span, :], dst.at[:, span, :], load_sem.at[k, i])
            if i < AHEAD:
                copy.start()
            pair.append(copy)
        loads.append(pair)
    control_copy = pltpu.make_async_copy(
        control_hbm.at[pl.ds(pl.multiple_of(own * quarter, 8), quarter), :], control_v, control_sem
    )
    control_copy.start()
    alpha_copy = pltpu.make_async_copy(alpha_hbm, alpha_ref, alpha_sem)
    alpha_copy.start()

    barrier = pltpu.get_barrier_semaphore()
    others = [(a, d) for a in range(groups) for d in range(tiles_n) if (a, d) != (0, 0)]
    others.sort(key=sum, reverse=True)
    others = [{"mem": lax.rem(me + a, groups), "col": lax.rem(tile + d, tiles_n)} for a, d in others]
    cube = [{"mem": other_core}, {"mem": other_chip}]
    step = 1
    while step < tiles_n:
        cube.append({"col": tile + step - 2 * step * lax.rem(lax.div(tile, step), 2)})
        step *= 2
    for peer in cube:
        pl.semaphore_signal(barrier, inc=1, device_id=peer)
    rounds = len(cube)
    passed = [0]

    def tell():
        k = passed[0]
        if 0 < k < rounds:
            pl.semaphore_wait(token.at[k - 1], 1)
        if k + 1 < rounds:
            pl.semaphore_signal(token.at[k], inc=1, device_id=cube[k + 1])
        passed[0] = k + 1

    def send(src, dst, out_sem, in_sem, peer):
        return pltpu.make_async_remote_copy(
            src_ref=src, dst_ref=dst, send_sem=out_sem, recv_sem=in_sem, device_id=peer
        )

    started = []

    def sums(i, dst):
        q, s = order[i]
        span = pl.ds(start(q, s), piece)
        for k, ref in enumerate((prior_v, out_ref)):
            loads[i][k].wait()
            total = ref[0, span, :]
            square = total * total
            for m in range(1, count):
                v = ref[m, span, :]
                total = total + v
                square = square + v * v
            dst[2 * k] = total
            dst[2 * k + 1] = square
            if i + AHEAD < len(order):
                loads[i + AHEAD][k].start()

    a_copies = {}

    def to_pair(k, s):
        sums(k * 2 * PARTS + 2 * s, send_a.at[k, s])
        if (k, s) == (0, 0):
            pl.semaphore_wait(barrier, len(cube))
        copy = send(
            send_a.at[k, s], recv_a.at[k, s], a_send.at[k, s], a_recv.at[k, s], {"mem": other_core}
        )
        copy.start()
        a_copies[k, s] = copy
        started.append(copy)

    x_copies = {}

    def to_chip(s):
        a_copies[0, s].wait_recv()
        sum_x[s] = sum_x[s] + recv_a[0, s]
        copy = send(sum_x.at[s], recv_x.at[s], x_send.at[s], x_recv.at[s], {"mem": other_chip})
        copy.start()
        x_copies[s] = copy
        started.append(copy)

    for s in range(PARTS):
        to_pair(0, s)
        sums(2 * s + 1, sum_x.at[s])
        if s >= 1:
            to_chip(s - 1)
            if s in (1, PARTS - 1):
                tell()
    for s in range(PARTS):
        to_pair(1, s)
        if s == 0:
            to_chip(PARTS - 1)
        sums(2 * PARTS + 2 * s + 1, sum_own.at[s])
        if s in (PARTS // 2, PARTS - 1):
            tell()

    row = lax.broadcasted_iota(jnp.int32, (quarter, LANES), 0) + start(own, 0)
    place = lax.shift_right_logical(row, 1) + tile * col_tiles
    lat_row = jnp.floor((place.astype(jnp.float32) + 0.5) * (1.0 / lat_tiles))
    weight_v[...] = jnp.cos((lat_row + 0.5) * (math.pi / lat_count) - math.pi / 2)
    alpha_copy.wait()
    level = lax.rem(lax.broadcasted_iota(jnp.int32, (piece, LANES), 0), 2)
    relax = jnp.where(level == 0, alpha_ref[0], alpha_ref[1])
    control_copy.wait()
    acc = [jnp.zeros((8, LANES), jnp.float32) for _ in range(4)]
    r_copies, d_copies = {}, {}
    for s in range(PARTS):
        a_copies[1, s].wait_recv()
        near = sum_own[s] + recv_a[1, s]
        x_copies[s].wait_recv()
        total = near + recv_x[s]
        mean_b = total[0] / members
        mean_a = total[2] / members
        var_b = jnp.maximum(total[1] - total[0] * mean_b, 0.0) / (members - 1)
        var_a = jnp.maximum(total[3] - total[2] * mean_a, 0.0) / (members - 1)
        spread_b = jnp.sqrt(var_b)
        spread_raw = jnp.sqrt(var_a)
        spread_a = jnp.sqrt(var_a + spread_floor)
        factor = (relax * spread_b + (1.0 - relax) * spread_a) / spread_a
        control = control_v[pl.ds(s * piece, piece), :]
        field[own, s, 0] = factor
        field[own, s, 1] = control - factor * mean_a
        r_copies[s] = send(
            field.at[own, s], field.at[own, s], r_send.at[s], r_recv.at[s], {"mem": other_chip}
        )
        d_copies[0, s] = send(
            field.at[own, s], field.at[own, s], d_send.at[0, s], d_recv.at[0, s], {"mem": other_core}
        )
        r_copies[s].start()
        d_copies[0, s].start()
        started += [r_copies[s], d_copies[0, s]]
        if s < PARTS - 1:
            tell()
        weight = weight_v[pl.ds(s * piece, piece), :]
        shift = control - mean_a
        terms = (weight * spread_b, weight * spread_raw, weight * factor * spread_raw, weight * shift * shift)
        for k, term in enumerate(terms):
            for i in range(piece // 8):
                acc[k] = acc[k] + term[8 * i : 8 * i + 8]

    sub = lax.broadcasted_iota(jnp.int32, (8, LANES), 0)
    lane = lax.broadcasted_iota(jnp.int32, (8, LANES), 1)
    tile_sum = jnp.zeros((8, LANES), jnp.float32)
    for k in range(4):
        v = acc[k] + pltpu.roll(acc[k], 4, 0)
        v = v + pltpu.roll(v, 2, 0)
        tile_sum = jnp.where(lax.div(sub, 2) == k, v, tile_sum)
    tile_sum = jnp.broadcast_to(jnp.sum(tile_sum, 1, keepdims=True), (8, LANES))
    tile_sum = jnp.where(lane == lax.div(sub, 2), tile_sum, 0.0)
    tile_sum = tile_sum + pltpu.roll(tile_sum, 4, 0)
    tile_sum = tile_sum + pltpu.roll(tile_sum, 2, 0)
    while passed[0] < rounds:
        tell()
    here = slots.at[me * tiles_n + tile]
    here[...] = tile_sum[:2]
    t_copies = []
    for i, peer in enumerate(others):
        copy = send(here, here, t_send.at[i], t_recv.at[i], peer)
        copy.start()
        t_copies.append(copy)
        started.append(copy)

    def apply(q, s):
        span = pl.ds(start(q, s), piece)
        factor = field[q, s, 0]
        offset = field[q, s, 1]
        for m in range(count):
            out_ref[m, span, :] = out_ref[m, span, :] * factor + offset

    for s in range(PARTS):
        apply(own, s)

    for s in range(PARTS):
        r_copies[s].wait_recv()
        d_copies[1, s] = send(
            field.at[mine_far, s], field.at[mine_far, s], d_send.at[1, s], d_recv.at[1, s], {"mem": other_core}
        )
        d_copies[1, s].start()
        started.append(d_copies[1, s])
        d_copies[0, s].wait_recv()
        apply(pair_near, s)
        apply(mine_far, s)
        if s >= 1:
            d_copies[1, s - 1].wait_recv()
            apply(pair_far, s - 1)
    d_copies[1, PARTS - 1].wait_recv()
    apply(pair_far, PARTS - 1)

    for copy in t_copies:
        copy.wait_recv()
    whole = slots[0]
    for t in range(1, groups * tiles_n):
        whole = whole + slots[t]
    whole = whole / weight_sum
    whole = jnp.where(lane[:2] == 3, jnp.sqrt(whole), whole)
    stats_ref[...] = whole[:, :4]

    for copy in started:
        copy.wait_send()


def to_tiles(array):
    lead, (levels, columns) = array.shape[:-2], array.shape[-2:]
    split = array.reshape(*lead, levels, columns // LANES, LANES)
    return jnp.swapaxes(split, -3, -2).reshape(*lead, levels * columns // LANES, LANES)


def from_tiles(array, levels):
    lead, rows = array.shape[:-2], array.shape[-2]
    split = array.reshape(*lead, rows // levels, levels, LANES)
    return jnp.swapaxes(split, -3, -2).reshape(*lead, levels, rows // levels * LANES)


def local(groups, tiles_n, prior, posterior, control, rtps_alpha):
    count, levels, columns = prior.shape
    rows = levels * columns // LANES
    piece = rows // 4 // PARTS
    lat_count = columns * tiles_n // NLON
    weight_sum = NLON * math.fsum(
        math.cos((r + 0.5) * math.pi / lat_count - math.pi / 2) for r in range(lat_count)
    )
    sizes = (groups, tiles_n, columns // LANES, NLON // LANES, lat_count, weight_sum)
    f32 = jnp.float32
    dma = pltpu.SemaphoreType.DMA
    hbm = pl.BlockSpec(memory_space=pl.ANY)
    analysis, stats = pl.pallas_call(
        functools.partial(kernel, sizes),
        out_shape=(
            pltpu.VMEM((count, rows, LANES), f32),
            pltpu.VMEM((levels, 4), f32),
        ),
        in_specs=[hbm, hbm, hbm, hbm],
        out_specs=(pl.BlockSpec(memory_space=pltpu.VMEM), pl.BlockSpec(memory_space=pltpu.VMEM)),
        scratch_shapes=[
            pltpu.VMEM((count, rows, LANES), f32),
            pltpu.VMEM((rows // 4, LANES), f32),
            pltpu.VMEM((2, PARTS, 4, piece, LANES), f32),
            pltpu.VMEM((2, PARTS, 4, piece, LANES), f32),
            pltpu.VMEM((PARTS, 4, piece, LANES), f32),
            pltpu.VMEM((PARTS, 4, piece, LANES), f32),
            pltpu.VMEM((PARTS, 4, piece, LANES), f32),
            pltpu.VMEM((4, PARTS, 2, piece, LANES), f32),
            pltpu.VMEM((groups * tiles_n, levels, LANES), f32),
            pltpu.VMEM((rows // 4, LANES), f32),
            pltpu.SMEM((levels,), f32),
            dma,
            dma((2, 4 * PARTS)),
            dma,
            dma((2, PARTS)),
            dma((2, PARTS)),
            dma((PARTS,)),
            dma((PARTS,)),
            dma((PARTS,)),
            dma((PARTS,)),
            dma((2, PARTS)),
            dma((2, PARTS)),
            dma((groups * tiles_n - 1,)),
            dma((groups * tiles_n - 1,)),
            pltpu.SemaphoreType.REGULAR((2 + tiles_n.bit_length(),)),
        ],
        compiler_params=pltpu.CompilerParams(collective_id=0, has_side_effects=True, vmem_limit_bytes=56 * 1024 * 1024),
    )(rtps_alpha, to_tiles(prior), to_tiles(posterior), to_tiles(control))
    return from_tiles(analysis, levels), stats.T


def solution(mesh):
    return jax.shard_map(
        functools.partial(local, mesh.shape["mem"], mesh.shape["col"]),
        mesh=mesh,
        in_specs=(P("mem", None, "col"), P("mem", None, "col"), P(None, "col"), P()),
        out_specs=(P("mem", None, "col"), P()),
        check_vma=False,
    )
```

profile of v0, /device:TPU:0, one launch (start us, length us, event | category | flops | bytes accessed | tf_op | source)
XLA Modules:
  0.0 24.6 jit_solution(15826443061511727145)
XLA Ops:
  0.6 20.8 %shard_map.59 = (f32[20,576,128]{2,1,0:T(8,128)S(1)}, f32[2,4]{1,0:T(2,128)S(1)}) custom-call(f32[2]{0:T(128)} %alpha_hbm.1, f32[20,576,128]{2,1,0:T(8,128)} %bitcast.23, f32[20,576,128]{2,1,0:T(8,128)} %bitcast.24, f32[576,128]{1,0:T(8,128)} %bitcast.25), custom_call_target="tpu_custom_call" | custom-call | tf_op jit(solution)/shard_map/pallas_call | solution.py:305
  21.4 2.6 %copy.12 = f32[20,2,36864]{2,1,0:T(2,128)} copy(f32[20,2,36864]{2,1,0:T(2,128)S(1)} %bitcast.21) | data formatting | bytes 11796480
  24.0 0.6 %copy.13 = f32[4,2]{0,1:T(2,128)} copy(f32[4,2]{0,1:T(2,128)S(1)} %bitcast.22) | data formatting | bytes 64
where the time goes:
time: 24.7 us; the launch traced here: 24.6 us
  Pallas kernels  20.8 us (84%)
  local copies, waits for them, and re-layouts  3.14 us (13%)
  between operations  0.64 us (3%)
    pallas_call x1, Pallas kernels, local(): pl.pallas_call(functools.partial(kernel, sizes), out_shape=(pltpu.VMEM((c...  20.8 us
    unnamed x2, local copies, waits for them, and re-layouts  3.14 us

commit v1 on v0

--- a/solution.py
+++ b/solution.py
@@ -278,6 +278,18 @@
         copy.wait_send()
 
 
+def write_out(groups, analysis_v, stats_v, analysis_hbm, stats_hbm, write_sem, stats_sem):
+    count = analysis_v.shape[0]
+    copies = [pltpu.make_async_copy(stats_v, stats_hbm, stats_sem)]
+    for g in range(groups):
+        span = pl.ds(g * (count // groups), count // groups)
+        copies.append(pltpu.make_async_copy(analysis_v.at[span], analysis_hbm.at[span], write_sem.at[g]))
+    for copy in copies[1:] + copies[:1]:
+        copy.start()
+    for copy in copies:
+        copy.wait()
+
+
 def to_tiles(array):
     lead, (levels, columns) = array.shape[:-2], array.shape[-2:]
     split = array.reshape(*lead, levels, columns // LANES, LANES)
@@ -339,6 +351,19 @@
         ],
         compiler_params=pltpu.CompilerParams(collective_id=0, has_side_effects=True, vmem_limit_bytes=56 * 1024 * 1024),
     )(rtps_alpha, to_tiles(prior), to_tiles(posterior), to_tiles(control))
+    vmem = pl.BlockSpec(memory_space=pltpu.VMEM)
+    writes = math.gcd(count, 10)
+    analysis, stats = pl.pallas_call(
+        functools.partial(write_out, writes),
+        out_shape=(
+            jax.ShapeDtypeStruct((count, rows, LANES), f32),
+            jax.ShapeDtypeStruct((levels, 4), f32),
+        ),
+        in_specs=[vmem, vmem],
+        out_specs=(hbm, hbm),
+        scratch_shapes=[dma((writes,)), dma],
+        compiler_params=pltpu.CompilerParams(vmem_limit_bytes=16 * 1024 * 1024),
+    )(analysis, stats)
     return from_tiles(analysis, levels), stats.T
 
 

time: 24.7 us -> 24.2 us (0.980)
  local copies, waits for them, and re-layouts: 3.14 us -> 0 us
  Pallas kernels: 20.8 us -> 23.4 us
    unnamed x2 -> x0, local copies, waits for them, and re-layouts: 3.14 us -> none
    pallas_call x0 -> x1, Pallas kernels: none -> 2.64 us  [local(): pl.pallas_call(functools.partial(write_out, writes), out_shape=(jax.Shape...]
where the time goes in v1:
time: 24.2 us; the launch traced here: 24.1 us
  Pallas kernels  23.4 us (97%)
  between operations  0.64 us (3%)
    pallas_call x1, Pallas kernels, local(): pl.pallas_call(functools.partial(kernel, sizes), out_shape=(pltpu.VMEM((c...  20.8 us
    pallas_call x1, Pallas kernels, local(): pl.pallas_call(functools.partial(write_out, writes), out_shape=(jax.Shape...  2.64 us

profile of v1, /device:TPU:0, one launch (start us, length us, event | category | flops | bytes accessed | tf_op | source)
XLA Modules:
  0.0 24.1 jit_solution(3672324470860164018)
XLA Ops:
  0.6 20.8 %shard_map.59 = (f32[20,576,128]{2,1,0:T(8,128)S(1)}, f32[2,4]{1,0:T(2,128)S(1)}) custom-call(f32[2]{0:T(128)} %alpha_hbm.1, f32[20,576,128]{2,1,0:T(8,128)} %bitcast.21, f32[20,576,128]{2,1,0:T(8,128)} %bitcast.22, f32[576,128]{1,0:T(8,128)} %bitcast.23), custom_call_target="tpu_custom_call" | custom-call | tf_op jit(solution)/shard_map/pallas_call | solution.py:317
  21.4 2.6 %shard_map.60 = (f32[20,576,128]{2,1,0:T(8,128)}, f32[2,4]{1,0:T(2,128)}) custom-call(f32[20,576,128]{2,1,0:T(8,128)S(1)} %get-tuple-element.6.analysis_v, f32[2,4]{1,0:T(2,128)S(1)} %get-tuple-element.7.stats_v), custom_call_target="tpu_custom_call" | custom-call | tf_op jit(solution)/shard_map/pallas_call | solution.py:356
